TPU v7x, 128 devices: a whole 4x4x4 slice. The times are simulated.
128 devices in a mesh: dp: 128 (over z, y, x, core).
Axes of the slice: x: 4, y: 4, z: 4, core: 2. Of those that a mesh axis runs over, the one named last changes fastest.
Arguments:
- hidden: bfloat16 [65536, 4096], P('dp')
- router_w: bfloat16 [4096, 128], replicated
- expert_idx: int32 [65536, 8], P('dp')
- gate_grad: float32 [65536, 8], P('dp')
Outputs:
- output 1: float32 [65536, 8], P('dp')
- output 2: float32 [], replicated
- output 3: bfloat16 [65536, 4096], P('dp')
- output 4: float32 [4096, 128], replicated
All inputs are finite; a program needn't handle non-finite values.
Results may differ from a plain program's by a relative error of at most 0.00786606.
Values sent between devices are 32-bit elements.
A program may use at most 1 GiB of HBM per device.

v0:
```python
import jax
import jax.numpy as jnp
from jax import lax
from jax.sharding import PartitionSpec as P

LOSS_ALPHA = 0.001


def gate_forward(hidden, router_w, expert_idx):
    logits = jnp.dot(hidden, router_w, preferred_element_type=jnp.float32)
    router_probs = jax.nn.softmax(logits, axis=-1)
    expert_ids = jnp.arange(router_w.shape[1], dtype=jnp.int32)
    idx_hits = expert_idx[:, :, None] == expert_ids[None, None, :]
    picked = jnp.sum(jnp.where(idx_hits, router_probs[:, None, :], 0.0), axis=2)
    pick_sum = jnp.sum(picked, axis=1, keepdims=True)
    return router_probs, idx_hits, pick_sum, picked / pick_sum


def logit_backward(router_probs, idx_hits, pick_sum, gate_probs, gate_grad, expert_freq, loss_scale, total_rows):
    num_experts = router_probs.shape[1]
    scaled_grad = loss_scale * gate_grad
    pick_grad = (scaled_grad - jnp.sum(scaled_grad * gate_probs, axis=1, keepdims=True)) / pick_sum
    aux_coef = loss_scale * LOSS_ALPHA * num_experts / total_rows
    prob_grad = jnp.sum(jnp.where(idx_hits, pick_grad[:, :, None], 0.0), axis=1) + aux_coef * expert_freq[None, :]
    logit_grad = router_probs * (prob_grad - jnp.sum(router_probs * prob_grad, axis=1, keepdims=True))
    return logit_grad.astype(jnp.bfloat16)


def solution(mesh):
    group_size = mesh.shape["dp"]

    def device_step(hidden, router_w, expert_idx, gate_grad):
        total_rows = hidden.shape[0] * group_size
        num_experts = router_w.shape[1]
        loss_scale = float(total_rows * num_experts * num_experts)
        router_probs, idx_hits, pick_sum, gate_probs = gate_forward(hidden, router_w, expert_idx)
        local_counts = jnp.sum(idx_hits, axis=(0, 1), dtype=jnp.float32)
        expert_freq = lax.psum(local_counts, "dp") / total_rows
        prob_mean = lax.psum(jnp.sum(router_probs, axis=0), "dp") / total_rows
        aux_loss = LOSS_ALPHA * num_experts * jnp.sum(expert_freq * prob_mean)
        grad_bf = logit_backward(router_probs, idx_hits, pick_sum, gate_probs, gate_grad, expert_freq, loss_scale, total_rows)
        hidden_grad = lax.dot_general(grad_bf, router_w, (((1,), (1,)), ((), ())), preferred_element_type=jnp.float32).astype(jnp.bfloat16)
        router_part = lax.dot_general(hidden, grad_bf, (((0,), (0,)), ((), ())), preferred_element_type=jnp.float32)
        router_grad = lax.psum(router_part, "dp")
        return gate_probs, aux_loss, hidden_grad, router_grad

    return jax.shard_map(device_step, mesh=mesh, in_specs=(P("dp", None), P(None, None), P("dp", None), P("dp", None)), out_specs=(P("dp", None), P(), P("dp", None), P(None, None)), check_vma=False)
```

profile of v0, /device:TPU:1, one launch (start us, length us, event | category | flops | bytes accessed | tf_op | source)
XLA Modules:
  0.0 257.0 jit_solution(291818462704592774)
XLA Ops:
  7.2 0.0 copy-start
  7.2 0.0 all-reduce.2.cloned.1.call-start
  7.2 0.9 copy.22
  8.2 0.3 copy-done
  8.4 3.7 %fusion.2 = (f32[512]{0:T(512)S(1)}, f32[512,128]{0,1:T(8,128)S(1)}) fusion(bf16[512,4096]{1,0:T(8,128)(2,1)} %param.4, bf16[4096,128]{1,0:T(8,128)(2,1)S(1)} %copy-done), kind=kOutput, calls=%fused_computation.17 | convolution fusion | flops 536935936 | bytes 5507072 | tf_op jit(solution)/shard_map/dot_general | solution.py:10
  12.1 0.0 copy-start.1
  12.1 0.1 fusion.1
  12.2 0.1 fusion
  12.3 0.1 copy.23
  12.4 8.0 %select_reduce_fusion = (f32[512]{0:T(512)S(1)}, f32[512,8]{1,0:T(8,128)S(1)}) fusion(f32[512,128]{1,0:T(8,128)S(1)} %copy.23, s32[512,8]{1,0:T(8,128)S(1)} %copy.22), kind=kLoop, calls=%fused_computation.2 | loop fusion | flops 2092544 | bytes 296960 | tf_op jit(solution)/shard_map/reduce_sum | solution.py:15
  20.3 0.1 copy.24
  20.4 0.0 copy-done.1
  20.4 0.6 multiply_reduce_fusion.1
  21.1 0.1 copy.25
  21.2 2.9 %select_reduce_fusion.2 = (f32[512,128]{1,0:T(8,128)S(1)}, f32[128]{0:T(128)S(1)}) fusion(f32[512,8]{1,0:T(8,128)S(1)} %copy.25, s32[512,8]{1,0:T(8,128)S(1)} %copy.22), kind=kLoop, calls=%fused_computation.4 | loop fusion | flops 3080064 | bytes 295424 | tf_op jit(solution)/shard_map/reduce_sum | solution.py:24
  24.1 0.1 copy.26
  24.2 68.7 %psum.21 = f32[128]{0:T(128)S(1)} all-reduce(f32[128]{0:T(128)S(1)} %get-tuple-element.21), channel_id=1, replica_groups=mesh['dp'=128] {'dp'}, use_global_device_ids=true, to_apply=%region_5.6 | all-reduce | flops 128 | bytes 1024 | tf_op jit(solution)/shard_map/psum | solution.py:38
  92.9 0.1 multiply_reduce_fusion
  93.1 0.1 multiply_convert_fusion
  93.2 4.2 %convolution_bitcast_fusion = f32[4096,128]{0,1:T(8,128)} fusion(bf16[512,128]{0,1:T(8,128)(2,1)S(1)} %multiply_convert_fusion, bf16[512,4096]{1,0:T(8,128)(2,1)} %param.4), kind=kOutput, calls=%fused_computation.1 | convolution fusion | flops 536870912 | bytes 6422528 | tf_op jit(solution)/shard_map/dot_general | solution.py:43
  97.4 0.0 all-reduce.2.cloned.1.call-update
  97.5 62.7 %psum.22 = f32[128]{0:T(128)S(1)} all-reduce(f32[128]{0:T(128)S(1)} %get-tuple-element.19), channel_id=1, replica_groups=mesh['dp'=128] {'dp'}, use_global_device_ids=true, to_apply=%region_7.8 | all-reduce | flops 128 | bytes 1024 | tf_op jit(solution)/shard_map/psum | solution.py:39
  160.1 0.6 multiply_reduce_fusion.2
  161.4 3.3 %convolution_convert_fusion = bf16[512,4096]{1,0:T(8,128)(2,1)} fusion(bf16[512,128]{0,1:T(8,128)(2,1)S(1)} %multiply_convert_fusion, bf16[4096,128]{1,0:T(8,128)(2,1)S(1)} %copy-done), kind=kOutput, calls=%fused_computation | convolution fusion | flops 538968064 | bytes 5373952 | tf_op jit(solution)/shard_map/dot_general | solution.py:42
  164.7 81.5 %all-reduce.2.cloned.1.call-done = f32[4096,128]{0,1:T(8,128)} async-done(((f32[4096,128]{0,1:T(8,128)}), f32[4096,128]{0,1:T(8,128)}) %all-reduce.2.cloned.1.call-update) | async-done | bytes 2097168 | tf_op jit(solution)/shard_map/psum | solution.py:44
  246.2 2.9 %copy.27 = f32[4096,128]{1,0:T(8,128)} copy(f32[4096,128]{0,1:T(8,128)} %all-reduce.2.cloned.1.call-done) | data formatting | bytes 4194304
  (2 shorter events, 0.0 us)
Async XLA Ops:
  7.2 1.2 copy-start
  7.2 239.0 %all-reduce.2.cloned.1.call-start = ((), (), s32[]{:S(2)}) async-start(), calls=%async_computation | async-start | bytes 4194304 | tf_op jit(solution)/shard_map/psum | solution.py:44
  12.1 8.3 %copy-start.1 = (f32[512,8]{0,1:T(8,128)S(1)}, f32[512,8]{0,1:T(8,128)}, u32[]{:S(2)}) copy-start(f32[512,8]{0,1:T(8,128)} %param.7) | copy-start | bytes 49156
Sparse Core Ops, SparseCore 0:
  97.6 148.5 all-reduce.1
where the time goes:
time: 258 us; the launch traced here: 257 us
  blocking collectives  131 us (51%)
  waiting for transfers between devices  81.5 us (32%)
  between operations  15.9 us (6%)
  other arithmetic  12.4 us (5%)
  matrix products  11.2 us (4%)
  local copies, waits for them, and re-layouts  4.54 us (2%)
    psum x1, waiting for transfers between devices, device_step(): router_grad = lax.psum(router_part, 'dp')  81.5 us
    psum x1, blocking collectives, device_step(): expert_freq = lax.psum(local_counts, 'dp') / total_rows  68.7 us
    psum x1, blocking collectives, device_step(): prob_mean = lax.psum(jnp.sum(router_probs, axis=0), 'dp') / total_rows  62.7 us
    reduce_sum x1, other arithmetic, gate_forward(): pick_sum = jnp.sum(picked, axis=1, keepdims=True)  7.95 us
  transfers between devices with their start and end apart: 1, of which 1 were waited for; matrix products, arithmetic and copies ran while one was open for 2% of the time, Pallas kernels for 0%

commit v1 on v0

v1 whole, which is shorter than its diff:
```python
import jax
import jax.numpy as jnp
from jax import lax
from jax.experimental import pallas as pl
from jax.experimental.pallas import tpu as pltpu
from jax.sharding import PartitionSpec as P

LOSS_ALPHA = 0.001
MESH = pl.DeviceIdType.MESH
AXIS = "dp"
RING = 4
STRIDES = (2, 8, 32)
REGIONS = ((0, 768), (768, 640), (1408, 640))
CHUNKS = 4
F32 = jnp.float32
BF16 = jnp.bfloat16


def peers_of(me, stride):
    pos = lax.rem(me // stride, RING)
    out = []
    for r in (1, 2, 3):
        q = lax.rem(pos + r, RING)
        out.append((me + (q - pos) * stride, q))
    return pos, out


def make_kernel(tokens, width, experts, top_k, total_rows, loss_scale):
    half = width // 2
    kc = width // CHUNKS
    aux_scale = LOSS_ALPHA * experts / total_rows
    aux_coef = loss_scale * LOSS_ALPHA * experts / total_rows

    def kernel(hid_hbm, w_hbm, idx_hbm, gg_hbm, gate_ref, aux_ref, hg_ref, rg_ref,
               hid, w, idx, gg, probs, base, own, give, take, cnt, cnt_in, aux, aux_in,
               r1a, r1b, r1c, r2a, r2b, r2c, r3a, r3b, r3c, s1a, s1b, s1c, s2a, s2b, s2c,
               load_sem, send_sem, recv_sem):
        me = lax.axis_index(AXIS)
        core = lax.rem(me, 2)
        partner = me + 1 - 2 * core
        used = [0]
        sends = []

        def remote(src, dst, peer):
            n = used[0]
            used[0] += 1
            cp = pltpu.make_async_remote_copy(
                src_ref=src, dst_ref=dst, send_sem=send_sem.at[n], recv_sem=recv_sem.at[n],
                device_id=(peer,), device_id_type=MESH)
            sends.append(cp)
            return cp

        loads = [pltpu.make_async_copy(idx_hbm, idx, load_sem.at[0]),
                 pltpu.make_async_copy(gg_hbm, gg, load_sem.at[1])]
        for i in range(CHUNKS):
            loads.append(pltpu.make_async_copy(w_hbm.at[pl.ds(i * kc, kc)], w.at[pl.ds(i * kc, kc)], load_sem.at[2 + 2 * i]))
            loads.append(pltpu.make_async_copy(hid_hbm.at[:, pl.ds(i * kc, kc)], hid.at[:, pl.ds(i * kc, kc)], load_sem.at[3 + 2 * i]))
        for cp in loads:
            cp.start()

        barrier = pltpu.get_barrier_semaphore()
        greet = [partner]
        for stride in STRIDES:
            greet += [peer for peer, _ in peers_of(me, stride)[1]]
        for peer in greet:
            pl.semaphore_signal(barrier, inc=1, device_id=(peer,), device_id_type=MESH)

        loads[0].wait()
        expert = lax.broadcasted_iota(jnp.int32, (experts, tokens), 0)
        hits = jnp.zeros((experts, tokens), F32)
        for j in range(top_k):
            hits = hits + jnp.where(expert == idx[j:j + 1, :], 1.0, 0.0)
        cnt[0] = lax.dot_general(jnp.ones((8, tokens), BF16), hits.astype(BF16),
                                 (((1,), (1,)), ((), ())), preferred_element_type=F32)
        pl.semaphore_wait(barrier, len(greet))

        def tile_start(src, dst, level):
            if level == 0:
                cps = [remote(src.at[0], dst.at[0], partner)]
            else:
                cps = [remote(src.at[level], dst.at[3 * level - 2 + 2 - r], peer)
                       for r, (peer, _) in enumerate(peers_of(me, STRIDES[level - 1])[1])]
            for cp in cps:
                cp.start()
            return cps

        def tile_finish(src, dst, level, cps):
            for cp in cps:
                cp.wait_recv()
            if level == 0:
                return src[0] + dst[0]
            b = 3 * level - 2
            return (src[level] + dst[b + 1]) + (dst[b] + dst[b + 2])

        flight = tile_start(cnt, cnt_in, 0)
        logits = jnp.zeros((tokens, experts), F32)
        for i in range(CHUNKS):
            loads[2 + 2 * i].wait()
            loads[3 + 2 * i].wait()
            logits = logits + jnp.dot(hid[:, i * kc:(i + 1) * kc], w[i * kc:(i + 1) * kc, :], preferred_element_type=F32)
            if i < 3:
                cnt[i + 1] = tile_finish(cnt, cnt_in, i, flight)
                flight = tile_start(cnt, cnt_in, i + 1)

        lt = logits.T
        e = jnp.exp(lt - jnp.max(lt, axis=0, keepdims=True))
        p = e * (1.0 / jnp.sum(e, axis=0, keepdims=True))
        probs[...] = p
        picked = jnp.concatenate(
            [jnp.sum(jnp.where(expert == idx[j:j + 1, :], p, 0.0), axis=0, keepdims=True) for j in range(top_k)], axis=0)
        inv_sum = 1.0 / jnp.sum(picked, axis=0, keepdims=True)
        gate = picked * inv_sum
        gate_ref[...] = gate
        loads[1].wait()
        sg = loss_scale * gg[...]
        pick_grad = (sg - jnp.sum(sg * gate, axis=0, keepdims=True)) * inv_sum
        pg = jnp.zeros((experts, tokens), F32)
        for j in range(top_k):
            pg = pg + jnp.where(expert == idx[j:j + 1, :], pick_grad[j:j + 1, :], 0.0)
        base[...] = pg

        total = tile_finish(cnt, cnt_in, 3, flight)
        freq = jnp.broadcast_to(total[0:1, :], (experts, experts)).T * (1.0 / total_rows)
        freq = jnp.concatenate([freq] * (tokens // experts), axis=1)
        p = probs[...]
        pf = jnp.sum(p * freq, axis=0, keepdims=True)
        pg = base[...] + aux_coef * freq
        lg = p * (pg - jnp.sum(p * pg, axis=0, keepdims=True))
        gt = lg.astype(BF16)
        aux[0] = jnp.broadcast_to(sum(pf[:, i * 128:(i + 1) * 128] for i in range(tokens // 128)), (8, 128))
        aux_flight = tile_start(aux, aux_in, 0)

        away = pl.multiple_of((1 - core) * half, 128)
        mine = pl.multiple_of(core * half, 128)
        d2d = []
        for lo, n in REGIONS:
            part = jnp.dot(gt, hid[:, pl.ds(pl.multiple_of(away + lo, 128), n)], preferred_element_type=F32)
            give[pl.ds(lo, n)] = part.T
            cp = remote(give.at[pl.ds(lo, n)], take.at[pl.ds(lo, n)], partner)
            cp.start()
            d2d.append(cp)

        r1, r2, r3 = (r1a, r1b, r1c), (r2a, r2b, r2c), (r3a, r3b, r3c)
        s1, s2 = (s1a, s1b, s1c), (s2a, s2b, s2c)

        def order(k):
            out = []
            for level in range(3):
                a, b = STRIDES[(k + level) % 3], STRIDES[(k + level + 1) % 3]
                out.append(a * (1 - core) + b * core)
            return out

        plan = []
        for k, (lo, n) in enumerate(REGIONS):
            strides = order(k)
            plan.append((lo, n // 4, n // 16) + tuple(peers_of(me, s) for s in strides))

        rs1 = []
        for k, (lo, n) in enumerate(REGIONS):
            part = jnp.dot(gt, hid[:, pl.ds(pl.multiple_of(mine + lo, 128), n)], preferred_element_type=F32)
            d2d[k].wait_recv()
            own[pl.ds(lo, n)] = part.T + take[pl.ds(lo, n)]
            _, c1, c2, (pos1, peers1), _, _ = plan[k]
            cps = []
            for r, (peer, q) in enumerate(peers1):
                cp = remote(own.at[pl.ds(pl.multiple_of(lo + q * c1, 8), c1)], r1[k].at[2 - r], peer)
                cp.start()
                cps.append(cp)
            rs1.append(cps)
        aux[1] = tile_finish(aux, aux_in, 0, aux_flight)
        aux_flight = tile_start(aux, aux_in, 1)

        g = lg.T.astype(BF16)
        for i in range(CHUNKS):
            hg_ref[:, i * kc:(i + 1) * kc] = lax.dot_general(
                g, w[i * kc:(i + 1) * kc, :], (((1,), (1,)), ((), ())), preferred_element_type=F32).astype(BF16)

        rs2 = []
        for k in range(3):
            lo, c1, c2, (pos1, peers1), (pos2, peers2), _ = plan[k]
            for cp in rs1[k]:
                cp.wait_recv()
            s1[k][...] = (own[pl.ds(pl.multiple_of(lo + pos1 * c1, 8), c1)] + r1[k][1]) + (r1[k][0] + r1[k][2])
            cps = []
            for r, (peer, q) in enumerate(peers2):
                cp = remote(s1[k].at[pl.ds(pl.multiple_of(q * c2, 8), c2)], r2[k].at[2 - r], peer)
                cp.start()
                cps.append(cp)
            rs2.append(cps)
        aux[2] = tile_finish(aux, aux_in, 1, aux_flight)
        aux_flight = tile_start(aux, aux_in, 2)

        b3 = []
        for k in range(3):
            lo, c1, c2, _, (pos2, _), (_, peers3) = plan[k]
            for cp in rs2[k]:
                cp.wait_recv()
            s2[k][...] = (s1[k][pl.ds(pl.multiple_of(pos2 * c2, 8), c2)] + r2[k][1]) + (r2[k][0] + r2[k][2])
            cps = []
            for r, (peer, q) in enumerate(peers3):
                cp = remote(s2[k], r3[k].at[2 - r], peer)
                cp.start()
                cps.append(cp)
            b3.append(cps)
        aux[3] = tile_finish(aux, aux_in, 2, aux_flight)
        aux_flight = tile_start(aux, aux_in, 3)

        ag2 = []
        for k in range(3):
            lo, c1, c2, (pos1, _), (pos2, peers2), _ = plan[k]
            for cp in b3[k]:
                cp.wait_recv()
            at = pl.ds(pl.multiple_of(mine + lo + pos1 * c1 + pos2 * c2, 8), c2)
            rg_ref[at] = (s2[k][...] + r3[k][1]) + (r3[k][0] + r3[k][2])
            cps = []
            for peer, q in peers2:
                cp = remote(rg_ref.at[at], rg_ref.at[at], peer)
                cp.start()
                cps.append(cp)
            ag2.append(cps)
        total_aux = tile_finish(aux, aux_in, 3, aux_flight)
        aux_ref[...] = jnp.broadcast_to(aux_scale * jnp.sum(total_aux[0:1, :], axis=1, keepdims=True), (8, 128))

        ag1, back = [], []
        for k in range(3):
            lo, c1, c2, (pos1, peers1), _, _ = plan[k]
            for cp in ag2[k]:
                cp.wait_recv()
            at = pl.ds(pl.multiple_of(mine + lo + pos1 * c1, 8), c1)
            cps = []
            for peer, q in peers1:
                cp = remote(rg_ref.at[at], rg_ref.at[at], peer)
                cp.start()
                cps.append(cp)
            ag1.append(cps)
            cp = remote(rg_ref.at[at], rg_ref.at[at], partner)
            cp.start()
            back.append(cp)
        for k in range(3):
            lo, c1, c2, (pos1, peers1), _, _ = plan[k]
            for r in range(3):
                ag1[k][r].wait_recv()
                q = lax.rem(pos1 + RING - (r + 1), RING)
                at = pl.ds(pl.multiple_of(mine + lo + q * c1, 8), c1)
                cp = remote(rg_ref.at[at], rg_ref.at[at], partner)
                cp.start()
                back.append(cp)
        for cp in back:
            cp.wait_recv()
        for cp in sends:
            cp.wait_send()

    return kernel


def solution(mesh):
    group_size = mesh.shape[AXIS]

    def device_step(hidden, router_w, expert_idx, gate_grad):
        tokens, width = hidden.shape
        experts, top_k = router_w.shape[1], expert_idx.shape[1]
        total_rows = tokens * group_size
        loss_scale = float(total_rows * experts * experts)
        half = width // 2
        vmem = pl.BlockSpec(memory_space=pltpu.VMEM)
        hbm = pl.BlockSpec(memory_space=pltpu.HBM)
        n_sems = 100
        scratch = [
            pltpu.VMEM((tokens, width), BF16), pltpu.VMEM((width, experts), BF16),
            pltpu.VMEM((top_k, tokens), jnp.int32), pltpu.VMEM((top_k, tokens), F32),
            pltpu.VMEM((experts, tokens), F32), pltpu.VMEM((experts, tokens), F32),
            pltpu.VMEM((half, experts), F32), pltpu.VMEM((half, experts), F32), pltpu.VMEM((half, experts), F32),
            pltpu.VMEM((4, 8, 128), F32), pltpu.VMEM((10, 8, 128), F32),
            pltpu.VMEM((4, 8, 128), F32), pltpu.VMEM((10, 8, 128), F32),
        ]
        scratch += [pltpu.VMEM((3, n // 4, experts), F32) for _, n in REGIONS]
        scratch += [pltpu.VMEM((3, n // 16, experts), F32) for _, n in REGIONS]
        scratch += [pltpu.VMEM((3, n // 16, experts), F32) for _, n in REGIONS]
        scratch += [pltpu.VMEM((n // 4, experts), F32) for _, n in REGIONS]
        scratch += [pltpu.VMEM((n // 16, experts), F32) for _, n in REGIONS]
        scratch += [pltpu.SemaphoreType.DMA((2 + 2 * CHUNKS,)), pltpu.SemaphoreType.DMA((n_sems,)), pltpu.SemaphoreType.DMA((n_sems,))]
        gate, aux, hg, rg = pl.pallas_call(
            make_kernel(tokens, width, experts, top_k, total_rows, loss_scale),
            out_shape=(jax.ShapeDtypeStruct((top_k, tokens), F32), jax.ShapeDtypeStruct((8, 128), F32),
                       jax.ShapeDtypeStruct((tokens, width), BF16), jax.ShapeDtypeStruct((width, experts), F32)),
            in_specs=[hbm, hbm, hbm, hbm],
            out_specs=(vmem, vmem, vmem, vmem),
            scratch_shapes=scratch,
            compiler_params=pltpu.CompilerParams(collective_id=0, has_side_effects=True, vmem_limit_bytes=40 * 1024 * 1024),
            name="router",
        )(*[pltpu.with_memory_space_constraint(x, pltpu.HBM) for x in (hidden, router_w, expert_idx.T, gate_grad.T)])
        return gate.T, aux[0, 0], hg, rg

    return jax.shard_map(device_step, mesh=mesh, in_specs=(P("dp", None), P(None, None), P("dp", None), P("dp", None)), out_specs=(P("dp", None), P(), P("dp", None), P(None, None)), check_vma=False)
```

time: 258 us -> 53.9 us (0.21)
  blocking collectives: 131 us -> 0 us
  waiting for transfers between devices: 81.5 us -> 0 us
  Pallas kernels: 0 us -> 48.7 us
  between operations: 15.9 us -> 0.64 us
  other arithmetic: 12.4 us -> 0 us
  matrix products: 11.2 us -> 0 us
    psum x2 -> x0, blocking collectives: 131 us -> none  [the longest x1 68.7 us: device_step(): expert_freq = lax.psum(local_counts, 'dp') / total_rows]
    psum x1 -> x0, waiting for transfers between devices: 81.5 us -> none  [device_step(): router_grad = lax.psum(router_part, 'dp')]
    pallas_call x0 -> x1, Pallas kernels: none -> 48.7 us  [device_step(): pl.pallas_call(make_kernel(tokens, width, experts, top_k, total_rows, los...]
    reduce_sum x6 -> x0, other arithmetic: 12.3 us -> none  [the longest x1 7.95 us: gate_forward(): pick_sum = jnp.sum(picked, axis=1, keepdims=True)]
    dot_general x3 -> x0, matrix products: 11.2 us -> none  [the longest x1 4.23 us: device_step(): lax.dot_general(hidden, grad_bf, (((0,), (0,)), ((), ())), preferred_elem...]
  transfers between devices with their start and end apart: 1 -> 0, of which waited for: 1 -> 0; matrix products, arithmetic and copies ran while one was open for 2% -> 0% of each run, Pallas kernels for 0% -> 0%
where the time goes in v1:
time: 53.9 us; the launch traced here: 53.8 us
  Pallas kernels  48.7 us (90%)
  local copies, waits for them, and re-layouts  4.45 us (8%)
  between operations  0.64 us (1%)
    pallas_call x1, Pallas kernels, device_step(): pl.pallas_call(make_kernel(tokens, width, experts, top_k, total_rows, los...  48.7 us
    unnamed x3, local copies, waits for them, and re-layouts  3.94 us

profile of v1, /device:TPU:1, one launch (start us, length us, event | category | flops | bytes accessed | tf_op | source)
XLA Modules:
  0.0 53.8 jit_solution(3642358252105488460)
XLA Ops:
  0.6 48.7 %router.1 = (f32[8,512]{1,0:T(8,128)S(1)}, f32[8,128]{1,0:T(8,128)S(1)}, bf16[512,4096]{1,0:T(8,128)(2,1)S(1)}, f32[4096,128]{1,0:T(8,128)S(1)}) custom-call(bf16[512,4096]{1,0:T(8,128)(2,1)} %hid_hbm.1, bf16[4096,128]{1,0:T(8,128)(2,1)} %w_hbm.1, s32[8,512]{1,0:T(8,128)} %bitcast.5, f32[8,512]{1,0:T(8,128)} %bitcast.6), custom_call_target="tpu_custom_call" | custom-call | tf_op jit(solution)/shard_map/router/pallas_call | solution.py:282
  49.3 0.5 slice.3
  49.8 0.6 %copy.11 = f32[512,8]{0,1:T(8,128)} copy(f32[512,8]{0,1:T(8,128)S(1)} %bitcast.4) | data formatting | bytes 32768
  50.4 2.0 %copy.12 = bf16[512,4096]{1,0:T(8,128)(2,1)} copy(bf16[512,4096]{1,0:T(8,128)(2,1)S(1)} %get-tuple-element.18) | data formatting | bytes 8388608
  52.4 1.3 %copy.13 = f32[4096,128]{1,0:T(8,128)} copy(f32[4096,128]{1,0:T(8,128)S(1)} %get-tuple-element.19) | data formatting | bytes 4194304
